TPU v7x, 256 devices: a whole 4x4x8 slice. The times are simulated.
256 devices in a mesh: row: 8 (over y, z_lo), col: 4 (over z_hi), depth: 8 (over x, core).
Axes of the slice: x: 4, y: 4, z: 8 (z_hi: 4, z_lo: 2; z = z_hi * 2 + z_lo), core: 2. Of those that a mesh axis runs over, the one named last changes fastest.
Arguments:
- grad_out: bfloat16 [2048, 6144], P('depth', 'col'), may hold values from -6 to 6
- pre_act: bfloat16 [2048, 24576], P('depth', 'row'), may hold values from -8 to 8
- down_weight: bfloat16 [24576, 6144], P(('row', 'depth'), 'col'), may hold values from -0.109375 to 0.109375
Outputs:
- grad_pre: bfloat16 [2048, 24576], P('depth', 'row')
- grad_weight: bfloat16 [24576, 6144], P(('row', 'depth'), 'col')
All inputs are finite; a program needn't handle non-finite values.
Results may differ from a plain program's by a relative error of at most 0.0066.
Values may be sent and summed in bfloat16 or wider, within the bound.
A program may use at most 64 MiB of HBM per device.

v0:
```python
import jax
import jax.numpy as jnp
from jax import lax
from jax.sharding import PartitionSpec as P

sqrt_two_pi = 0.7978845608028654
cubic_coeff = 0.044715


def split_up(array, dim, count):
    dims = array.shape
    pieces = array.reshape(*dims[:dim], count, dims[dim] // count, *dims[dim + 1 :])
    return jnp.moveaxis(pieces, dim, 0)


def sum_at_owner(array, axis, dim):
    count = lax.axis_size(axis)
    pieces = lax.all_to_all(split_up(array, dim, count), axis, 0, 0, tiled=True)
    return jnp.sum(pieces.astype(jnp.float32), axis=0)


def sent_to_all(array, axis):
    count = lax.axis_size(axis)
    return lax.all_to_all(
        jnp.broadcast_to(array[None], (count, *array.shape)), axis, 0, 0, tiled=True
    )


def laid_out(pieces, dim):
    dims = list(pieces.shape[1:])
    dims[dim] *= pieces.shape[0]
    return jnp.moveaxis(pieces, 0, dim).reshape(dims)


def collect(array, axis, dim):
    pieces = sent_to_all(array, axis)
    return laid_out(pieces, dim)


def gelu_value(preact):
    tangent = jnp.tanh(sqrt_two_pi * (preact + cubic_coeff * preact * preact * preact))
    return 0.5 * preact * (1.0 + tangent)


def gelu_slope(preact):
    tangent = jnp.tanh(sqrt_two_pi * (preact + cubic_coeff * preact * preact * preact))
    inner = sqrt_two_pi * (1.0 + 3.0 * cubic_coeff * preact * preact)
    return 0.5 * (1.0 + tangent) + 0.5 * preact * (1.0 - tangent * tangent) * inner


def contract_last(left, right):
    return lax.dot_general(
        left, right, (((1,), (1,)), ((), ())), preferred_element_type=jnp.float32
    )


def contract_first(left, right):
    return lax.dot_general(
        left, right, (((0,), (0,)), ((), ())), preferred_element_type=jnp.float32
    )


def finish_rows(partial_value, preacts):
    share = sum_at_owner(partial_value.astype(jnp.bfloat16), "col", 0)
    height = share.shape[0]
    offset = lax.axis_index("col") * height
    pre_rows = lax.dynamic_slice_in_dim(preacts, offset, height, 0)
    pieces = (share * gelu_slope(pre_rows.astype(jnp.float32))).astype(jnp.bfloat16)
    return collect(pieces, "col", 0)


def on_device(grad_out, pre_act, down_weight):
    every_grad = lax.all_gather(grad_out, "depth", axis=0, tiled=True)
    own_pre = lax.all_to_all(pre_act, "depth", split_axis=1, concat_axis=0, tiled=True)
    partial_value = contract_last(every_grad, down_weight)
    local_grad = finish_rows(partial_value, own_pre)
    grad_pre = lax.all_to_all(local_grad, "depth", split_axis=0, concat_axis=1, tiled=True)
    own_act = gelu_value(own_pre.astype(jnp.float32)).astype(jnp.bfloat16)
    grad_weight = contract_first(own_act, every_grad).astype(jnp.bfloat16)
    return (grad_pre, grad_weight)


def solution(mesh):
    placed = (P("depth", "col"), P("depth", "row"), P(("row", "depth"), "col"))
    return jax.shard_map(
        on_device,
        mesh=mesh,
        in_specs=placed,
        out_specs=(P("depth", "row"), P(("row", "depth"), "col")),
        check_vma=False,
    )
```

profile of v0, /device:TPU:56, one launch (start us, length us, event | category | flops | bytes accessed | tf_op | source)
XLA Modules:
  0.0 198.6 jit_solution(504990352886837358)
XLA Ops:
  7.2 0.0 copy-start
  7.2 0.0 all-gather.2.cloned.1.call-start
  7.2 0.7 all-gather.2.cloned.1.call-update
  7.9 2.6 %copy.5 = bf16[256,3072]{0,1:T(8,128)(2,1)} copy(bf16[256,3072]{1,0:T(8,128)(2,1)} %param.4) | data formatting | bytes 3145728 | tf_op args[1]
  10.5 4.3 %all-to-all-start.1 = ((bf16[256,8,384]{0,2,1:T(8,128)(2,1)}), bf16[256,8,384]{0,2,1:T(8,128)(2,1)S(1)}, u32[]{:S(2)}, u32[]{:S(2)}) async-start(bf16[256,8,384]{0,2,1:T(8,128)(2,1)} %bitcast.12), calls=%async_computation.1 | async-start | bytes 3145728 | tf_op jit(solution)/shard_map/all_to_all | solution.py:74
  14.8 48.3 %all-gather.2.cloned.1.call-done = bf16[2048,1536]{1,0:T(8,128)(2,1)} async-done(((bf16[256,1536]{1,0:T(8,128)(2,1)}), bf16[2048,1536]{1,0:T(8,128)(2,1)}) %all-gather.2.cloned.1.call-update) | async-done | bytes 6291472 | tf_op jit(solution)/shard_map/all_gather | solution.py:73
  63.0 0.0 copy-done
  63.0 7.4 %convolution_convert_fusion.1 = bf16[2048,384]{1,0:T(8,128)(2,1)} fusion(bf16[2048,1536]{1,0:T(8,128)(2,1)} %all-gather.2.cloned.1.call-done, bf16[384,1536]{1,0:T(8,128)(2,1)S(1)} %copy-done), kind=kOutput, calls=%fused_computation.12 | convolution fusion | flops 2416705536 | bytes 9043968 | tf_op jit(solution)/shard_map/dot_general | solution.py:52
  70.4 0.0 all-to-all-done.1
  70.4 7.6 %all-to-all-start = ((bf16[4,512,384]{2,1,0:T(8,128)(2,1)}), bf16[4,512,384]{2,1,0:T(8,128)(2,1)}, u32[]{:S(2)}, u32[]{:S(2)}) async-start(bf16[4,512,384]{2,1,0:T(8,128)(2,1)} %bitcast.17), calls=%async_computation | async-start | bytes 3145728 | tf_op jit(solution)/shard_map/all_to_all | solution.py:18
  78.0 1.6 copy.6
  79.5 38.5 %all-to-all-done = bf16[4,512,384]{2,1,0:T(8,128)(2,1)} async-done(((bf16[4,512,384]{2,1,0:T(8,128)(2,1)}), bf16[4,512,384]{2,1,0:T(8,128)(2,1)}, u32[]{:S(2)}, u32[]{:S(2)}) %all-to-all-start) | async-done | bytes 1572896 | tf_op jit(solution)/shard_map/all_to_all | solution.py:18
  118.0 1.7 convert_reduce_fusion
  119.8 1.5 fusion.16
  121.3 0.1 broadcast_in_dim.2
  121.4 41.0 %all_to_all.48 = bf16[4,512,384]{2,1,0:T(8,128)(2,1)} all-to-all(bf16[4,512,384]{2,1,0:T(8,128)(2,1)S(1)} %broadcast_in_dim.2), channel_id=1, replica_groups=mesh['row'=8,'col'=4,'depth'=8] {'col'}, dimensions={0} | all-to-all | bytes 3145728 | tf_op jit(solution)/shard_map/all_to_all | solution.py:24
  162.5 3.6 %all-to-all-start.3 = ((bf16[8,256,384]{2,1,0:T(8,128)(2,1)}), bf16[8,256,384]{2,1,0:T(8,128)(2,1)S(1)}, u32[]{:S(2)}, u32[]{:S(2)}) async-start(bf16[8,256,384]{2,1,0:T(8,128)(2,1)} %bitcast.13), calls=%async_computation.3 | async-start | bytes 3145728 | tf_op jit(solution)/shard_map/all_to_all | solution.py:77
  166.1 7.0 %convolution_convert_fusion = bf16[384,1536]{1,0:T(8,128)(2,1)} fusion(bf16[2048,1536]{1,0:T(8,128)(2,1)} %all-gather.2.cloned.1.call-done, bf16[2048,384]{1,0:T(8,128)(2,1)} %bitcast.16), kind=kOutput, calls=%fused_computation.11 | convolution fusion | flops 2424373248 | bytes 9043968 | tf_op jit(solution)/shard_map/dot_general | solution.py:58
  173.0 14.5 %all-to-all-done.3 = bf16[8,256,384]{2,1,0:T(8,128)(2,1)S(1)} async-done(((bf16[8,256,384]{2,1,0:T(8,128)(2,1)}), bf16[8,256,384]{2,1,0:T(8,128)(2,1)S(1)}, u32[]{:S(2)}, u32[]{:S(2)}) %all-to-all-start.3) | async-done | bytes 1572896 | tf_op jit(solution)/shard_map/all_to_all | solution.py:77
  187.5 1.6 copy.7
  189.2 2.6 %copy.8 = bf16[256,3072]{1,0:T(8,128)(2,1)} copy(bf16[256,3072]{0,1:T(8,128)(2,1)} %bitcast.14) | data formatting | bytes 3145728
Async XLA Ops:
  7.2 55.9 %copy-start = (bf16[384,1536]{1,0:T(8,128)(2,1)S(1)}, bf16[384,1536]{1,0:T(8,128)(2,1)}, u32[]{:S(2)}) copy-start(bf16[384,1536]{1,0:T(8,128)(2,1)} %param.5) | copy-start | bytes 3538948
  7.2 55.9 %all-gather.2.cloned.1.call-start = ((), (), s32[]{:S(2)}) async-start(), calls=%async_computation.4 | async-start | bytes 7077888 | tf_op jit(solution)/shard_map/all_gather | solution.py:73
  10.5 59.9 %all-to-all-start.1 = ((bf16[256,8,384]{0,2,1:T(8,128)(2,1)}), bf16[256,8,384]{0,2,1:T(8,128)(2,1)S(1)}, u32[]{:S(2)}, u32[]{:S(2)}) async-start(bf16[256,8,384]{0,2,1:T(8,128)(2,1)} %bitcast.12), calls=%async_computation.1 | async-start | bytes 3145728 | tf_op jit(solution)/shard_map/all_to_all | solution.py:74
  70.4 47.6 %all-to-all-start = ((bf16[4,512,384]{2,1,0:T(8,128)(2,1)}), bf16[4,512,384]{2,1,0:T(8,128)(2,1)}, u32[]{:S(2)}, u32[]{:S(2)}) async-start(bf16[4,512,384]{2,1,0:T(8,128)(2,1)} %bitcast.17), calls=%async_computation | async-start | bytes 3145728 | tf_op jit(solution)/shard_map/all_to_all | solution.py:18
  162.5 25.1 %all-to-all-start.3 = ((bf16[8,256,384]{2,1,0:T(8,128)(2,1)}), bf16[8,256,384]{2,1,0:T(8,128)(2,1)S(1)}, u32[]{:S(2)}, u32[]{:S(2)}) async-start(bf16[8,256,384]{2,1,0:T(8,128)(2,1)} %bitcast.13), calls=%async_computation.3 | async-start | bytes 3145728 | tf_op jit(solution)/shard_map/all_to_all | solution.py:77
Sparse Core Ops, SparseCore 0:
  9.8 53.1 all-gather.1
where the time goes:
time: 199 us
  waiting for transfers between devices  102 us (51%)
  blocking collectives  41 us (21%)
  starting transfers between devices  15.5 us (8%)
  matrix products  14.4 us (7%)
  between operations  14.1 us (7%)
  local copies, waits for them, and re-layouts  8.49 us (4%)
  other arithmetic  3.26 us (2%)
    all_gather x1, waiting for transfers between devices, on_device(): every_grad = lax.all_gather(grad_out, 'depth', axis=0, tiled=True)  48.3 us
    all_to_all x1, blocking collectives, sent_to_all(): lax.all_to_all(jnp.broadcast_to(array[None], (count, *array.shape)), axis...  41 us
    all_to_all x1, waiting for transfers between devices, sum_at_owner(): pieces = lax.all_to_all(split_up(array, dim, count), axis, 0, 0, tiled=True)  38.5 us
    all_to_all x1, waiting for transfers between devices, on_device(): lax.all_to_all(local_grad, 'depth', split_axis=0, concat_axis=1, tiled=True)  14.5 us
    all_to_all x1, starting transfers between devices, sum_at_owner(): pieces = lax.all_to_all(split_up(array, dim, count), axis, 0, 0, tiled=True)  7.55 us
    dot_general x1, matrix products, contract_last(): lax.dot_general(left, right, (((1,), (1,)), ((), ())), preferred_element_...  7.39 us
    dot_general x1, matrix products, contract_first(): lax.dot_general(left, right, (((0,), (0,)), ((), ())), preferred_element_...  6.99 us
    unnamed x4, local copies, waits for them, and re-layouts  5.16 us
  transfers between devices with their start and end apart: 4, of which 3 were waited for; matrix products, arithmetic and copies ran while one was open for 9% of the time, Pallas kernels for 0%

commit v1 on v0

--- a/solution.py
+++ b/solution.py
@@ -70,7 +70,22 @@
 
 
 def on_device(grad_out, pre_act, down_weight):
-    every_grad = lax.all_gather(grad_out, "depth", axis=0, tiled=True)
+    size, place, rows = (lax.axis_size("depth"), lax.axis_index("depth"), grad_out.shape[0])
+    right_2 = [(i, (i + 1) % size) for i in range(size)]
+    downward = [(i, (i - 1) % size) for i in range(size)]
+    out = jnp.zeros((*grad_out.shape[:0], size * rows, *grad_out.shape[0 + 1 :]), grad_out.dtype)
+    out = lax.dynamic_update_slice_in_dim(out, grad_out, place * rows, axis=0)
+    from_left = from_right = grad_out
+    middle = size // 2
+    for step in range(1, middle + 1):
+        from_left = lax.ppermute(from_left, "depth", right_2)
+        out = lax.dynamic_update_slice_in_dim(out, from_left, (place - step) % size * rows, axis=0)
+        if step < size - middle:
+            from_right = lax.ppermute(from_right, "depth", downward)
+            out = lax.dynamic_update_slice_in_dim(
+                out, from_right, (place + step) % size * rows, axis=0
+            )
+    every_grad = out
     own_pre = lax.all_to_all(pre_act, "depth", split_axis=1, concat_axis=0, tiled=True)
     partial_value = contract_last(every_grad, down_weight)
     local_grad = finish_rows(partial_value, own_pre)

time: 199 us -> 191 us (0.960)
  between operations: 14.1 us -> 0.74 us
  starting transfers between devices: 15.5 us -> 27.3 us
  waiting for transfers between devices: 102 us -> 92.9 us
  local copies, waits for them, and re-layouts: 8.49 us -> 16.3 us
  matrix products: 14.4 us -> 11.5 us
  blocking collectives: 41 us -> 38.3 us
    all_gather x1 -> x0, waiting for transfers between devices: 48.3 us -> none  [on_device(): every_grad = lax.all_gather(grad_out, 'depth', axis=0, tiled=True)]
    ppermute x0 -> x7, waiting for transfers between devices: none -> 42.7 us  [the longest x4 28.1 us: on_device(): from_left = lax.ppermute(from_left, 'depth', right_2)]
    ppermute x0 -> x7, starting transfers between devices: none -> 8.98 us  [the longest x3 8.96 us: on_device(): from_right = lax.ppermute(from_right, 'depth', downward)]
    dynamic_update_slice x0 -> x8, local copies, waits for them, and re-layouts: none -> 3.86 us  [the longest x3 2.44 us: on_device(): lax.dynamic_update_slice_in_dim(out, from_right, (place + step) % size *...]
    unnamed x4 -> x12, local copies, waits for them, and re-layouts: 5.16 us -> 8.69 us
    all_to_all x1, starting transfers between devices: 3.58 us -> 6.52 us  [on_device(): lax.all_to_all(local_grad, 'depth', split_axis=0, concat_axis=1, tiled=True)]
    dot_general x1, matrix products: 7.39 us -> 4.5 us  [contract_last(): lax.dot_general(left, right, (((1,), (1,)), ((), ())), preferred_element_...]
    all_to_all x1, waiting for transfers between devices: 38.5 us -> 35.6 us  [sum_at_owner(): pieces = lax.all_to_all(split_up(array, dim, count), axis, 0, 0, tiled=True)]
  transfers between devices with their start and end apart: 4 -> 10, of which waited for: 3 -> 7; matrix products, arithmetic and copies ran while one was open for 9% -> 10% of each run, Pallas kernels for 0% -> 0%
where the time goes in v1:
time: 191 us; the launch traced here: 190 us
  waiting for transfers between devices  92.9 us (49%)
  blocking collectives  38.3 us (20%)
  starting transfers between devices  27.3 us (14%)
  local copies, waits for them, and re-layouts  16.3 us (9%)
  matrix products  11.5 us (6%)
  other arithmetic  3.24 us (2%)
    all_to_all x1, blocking collectives, sent_to_all(): lax.all_to_all(jnp.broadcast_to(array[None], (count, *array.shape)), axis...  38.3 us
    all_to_all x1, waiting for transfers between devices, sum_at_owner(): pieces = lax.all_to_all(split_up(array, dim, count), axis, 0, 0, tiled=True)  35.6 us
    ppermute x4, waiting for transfers between devices, on_device(): from_left = lax.ppermute(from_left, 'depth', right_2)  28.1 us
    ppermute x3, waiting for transfers between devices, on_device(): from_right = lax.ppermute(from_right, 'depth', downward)  14.7 us
    all_to_all x1, waiting for transfers between devices, on_device(): lax.all_to_all(local_grad, 'depth', split_axis=0, concat_axis=1, tiled=True)  14.6 us
    ppermute x3, starting transfers between devices, on_device(): from_right = lax.ppermute(from_right, 'depth', downward)  8.96 us
    unnamed x12, local copies, waits for them, and re-layouts  8.69 us
    all_to_all x1, starting transfers between devices, sum_at_owner(): pieces = lax.all_to_all(split_up(array, dim, count), axis, 0, 0, tiled=True)  7.56 us
  transfers between devices with their start and end apart: 10, of which 7 were waited for; matrix products, arithmetic and copies ran while one was open for 10% of the time, Pallas kernels for 0%

profile of v1, /device:TPU:56, one launch (start us, length us, event | category | flops | bytes accessed | tf_op | source)
XLA Modules:
  0.0 190.3 jit_solution(15819615060621878168)
XLA Ops:
  0.7 2.9 %collective-permute-start.1 = (bf16[256,1536]{1,0:T(8,128)(2,1)}, bf16[256,1536]{1,0:T(8,128)(2,1)}, u32[]{:S(2)}, u32[]{:S(2)}) collective-permute-start(bf16[256,1536]{1,0:T(8,128)(2,1)} %param.3), channel_id=1, source_target_pairs={{0,7},{1,0},{2,1},{3,2},{4,3},{5,4},{6,5},{7,6},{8,15},{9,8},{10,9... | collective-permute-start | bytes 2359304 | tf_op jit(solution)/shard_map/ppermute | solution.py:84
  3.6 9.9 %collective-permute-done = bf16[256,1536]{1,0:T(8,128)(2,1)S(1)} collective-permute-done((bf16[256,1536]{1,0:T(8,128)(2,1)}, bf16[256,1536]{1,0:T(8,128)(2,1)S(1)}, u32[]{:S(2)}, u32[]{:S(2)}) %collective-permute-start) | collective-permute-done | bytes 786464 | tf_op jit(solution)/shard_map/ppermute | solution.py:81
  13.5 3.1 %collective-permute-start.3 = (bf16[256,1536]{1,0:T(8,128)(2,1)}, bf16[256,1536]{1,0:T(8,128)(2,1)}, u32[]{:S(2)}, u32[]{:S(2)}) collective-permute-start(bf16[256,1536]{1,0:T(8,128)(2,1)} %collective-permute-done.1), channel_id=1, source_target_pairs={{0,7},{1,0},{2,1},{3,2},{4,3},{5,4},{6,5},{7,6},{8,15},{9,8},{10,9... | collective-permute-start | bytes 2359304 | tf_op jit(solution)/shard_map/ppermute | solution.py:84
  16.6 9.7 %collective-permute-done.2 = bf16[256,1536]{1,0:T(8,128)(2,1)} collective-permute-done((bf16[256,1536]{1,0:T(8,128)(2,1)S(1)}, bf16[256,1536]{1,0:T(8,128)(2,1)}, u32[]{:S(2)}, u32[]{:S(2)}) %collective-permute-start.2) | collective-permute-done | bytes 786464 | tf_op jit(solution)/shard_map/ppermute | solution.py:81
  26.2 2.6 %copy.5 = bf16[256,3072]{0,1:T(8,128)(2,1)} copy(bf16[256,3072]{1,0:T(8,128)(2,1)} %param.4) | data formatting | bytes 3145728 | tf_op args[1]
  28.8 4.2 %all-to-all-start.1 = ((bf16[256,8,384]{0,2,1:T(8,128)(2,1)}), bf16[256,8,384]{0,2,1:T(8,128)(2,1)S(1)}, u32[]{:S(2)}, u32[]{:S(2)}) async-start(bf16[256,8,384]{0,2,1:T(8,128)(2,1)} %bitcast.11), calls=%async_computation.1 | async-start | bytes 3145728 | tf_op jit(solution)/shard_map/all_to_all | solution.py:89
  33.0 0.4 broadcast_in_dim.4
  33.5 0.7 copy-done.2
  34.2 0.2 copy-done.4
  34.5 3.0 %collective-permute-start.5 = (bf16[256,1536]{1,0:T(8,128)(2,1)}, bf16[256,1536]{1,0:T(8,128)(2,1)S(1)}, u32[]{:S(2)}, u32[]{:S(2)}) collective-permute-start(bf16[256,1536]{1,0:T(8,128)(2,1)} %collective-permute-done.3), channel_id=1, source_target_pairs={{0,7},{1,0},{2,1},{3,2},{4,3},{5,4},{6,5},{7,6},{8,15},{9,8},{10,9... | collective-permute-start | bytes 2359304 | tf_op jit(solution)/shard_map/ppermute | solution.py:84
  37.4 1.2 constant_dynamic-update-slice_fusion.5
  38.6 3.8 %collective-permute-done.4 = bf16[256,1536]{1,0:T(8,128)(2,1)S(1)} collective-permute-done((bf16[256,1536]{1,0:T(8,128)(2,1)}, bf16[256,1536]{1,0:T(8,128)(2,1)S(1)}, u32[]{:S(2)}, u32[]{:S(2)}) %collective-permute-start.4) | collective-permute-done | bytes 786464 | tf_op jit(solution)/shard_map/ppermute | solution.py:81
  42.4 1.2 constant_dynamic-update-slice_fusion.4
  43.6 1.2 constant_dynamic-update-slice_fusion.3
  44.8 0.1 constant_dynamic-update-slice_fusion.2
  44.9 14.7 %collective-permute-done.5 = bf16[256,1536]{1,0:T(8,128)(2,1)S(1)} collective-permute-done((bf16[256,1536]{1,0:T(8,128)(2,1)}, bf16[256,1536]{1,0:T(8,128)(2,1)S(1)}, u32[]{:S(2)}, u32[]{:S(2)}) %collective-permute-start.5) | collective-permute-done | bytes 786464 | tf_op jit(solution)/shard_map/ppermute | solution.py:84
  59.5 0.1 constant_dynamic-update-slice_fusion.1
  59.6 4.8 %collective-permute-done.6 = bf16[256,1536]{1,0:T(8,128)(2,1)S(1)} collective-permute-done((bf16[256,1536]{1,0:T(8,128)(2,1)S(1)}, bf16[256,1536]{1,0:T(8,128)(2,1)S(1)}, u32[]{:S(2)}, u32[]{:S(2)}) %collective-permute-start.6) | collective-permute-done | bytes 786464 | tf_op jit(solution)/shard_map/ppermute | solution.py:81
  64.4 2.6 %copy-done.1 = bf16[2048,1536]{1,0:T(8,128)(2,1)} copy-done((bf16[2048,1536]{1,0:T(8,128)(2,1)}, bf16[2048,1536]{1,0:T(8,128)(2,1)S(1)}, u32[]{:S(2)}) %copy-start.1) | copy-done | bytes 6291480
  67.1 4.5 %convolution_convert_fusion.1 = bf16[2048,384]{1,0:T(8,128)(2,1)} fusion(bf16[2048,1536]{1,0:T(8,128)(2,1)S(1)} %constant_dynamic-update-slice_fusion, bf16[384,1536]{1,0:T(8,128)(2,1)S(1)} %copy-done), kind=kOutput, calls=%fused_computation.12 | convolution fusion | flops 2416705536 | bytes 9043968 | tf_op jit(solution)/shard_map/dot_general | solution.py:52
  71.6 7.6 %all-to-all-start = ((bf16[4,512,384]{2,1,0:T(8,128)(2,1)}), bf16[4,512,384]{2,1,0:T(8,128)(2,1)}, u32[]{:S(2)}, u32[]{:S(2)}) async-start(bf16[4,512,384]{2,1,0:T(8,128)(2,1)} %bitcast.17), calls=%async_computation | async-start | bytes 3145728 | tf_op jit(solution)/shard_map/all_to_all | solution.py:18
  79.1 1.6 copy.6
  80.7 35.6 %all-to-all-done = bf16[4,512,384]{2,1,0:T(8,128)(2,1)} async-done(((bf16[4,512,384]{2,1,0:T(8,128)(2,1)}), bf16[4,512,384]{2,1,0:T(8,128)(2,1)}, u32[]{:S(2)}, u32[]{:S(2)}) %all-to-all-start) | async-done | bytes 1572896 | tf_op jit(solution)/shard_map/all_to_all | solution.py:18
  116.3 1.7 convert_reduce_fusion
  118.0 1.5 fusion.16
  119.6 0.1 broadcast_in_dim.10
  119.7 38.3 %all_to_all.48 = bf16[4,512,384]{2,1,0:T(8,128)(2,1)} all-to-all(bf16[4,512,384]{2,1,0:T(8,128)(2,1)S(1)} %broadcast_in_dim.10), channel_id=1, replica_groups=mesh['row'=8,'col'=4,'depth'=8] {'col'}, dimensions={0} | all-to-all | bytes 3145728 | tf_op jit(solution)/shard_map/all_to_all | solution.py:24
  158.0 6.5 %all-to-all-start.3 = ((bf16[8,256,384]{2,1,0:T(8,128)(2,1)}), bf16[8,256,384]{2,1,0:T(8,128)(2,1)S(1)}, u32[]{:S(2)}, u32[]{:S(2)}) async-start(bf16[8,256,384]{2,1,0:T(8,128)(2,1)} %bitcast.13), calls=%async_computation.3 | async-start | bytes 3145728 | tf_op jit(solution)/shard_map/all_to_all | solution.py:92
  164.5 7.0 %convolution_convert_fusion = bf16[384,1536]{1,0:T(8,128)(2,1)} fusion(bf16[2048,1536]{1,0:T(8,128)(2,1)} %copy-done.1, bf16[2048,384]{1,0:T(8,128)(2,1)} %bitcast.16), kind=kOutput, calls=%fused_computation.11 | convolution fusion | flops 2424373248 | bytes 9043968 | tf_op jit(solution)/shard_map/dot_general | solution.py:58
  171.5 14.6 %all-to-all-done.3 = bf16[8,256,384]{2,1,0:T(8,128)(2,1)S(1)} async-done(((bf16[8,256,384]{2,1,0:T(8,128)(2,1)}), bf16[8,256,384]{2,1,0:T(8,128)(2,1)S(1)}, u32[]{:S(2)}, u32[]{:S(2)}) %all-to-all-start.3) | async-done | bytes 1572896 | tf_op jit(solution)/shard_map/all_to_all | solution.py:92
  186.0 1.7 copy.7
  187.7 2.6 %copy.8 = bf16[256,3072]{1,0:T(8,128)(2,1)} copy(bf16[256,3072]{0,1:T(8,128)(2,1)} %bitcast.14) | data formatting | bytes 3145728
  (17 shorter events, 0.2 us)
Async XLA Ops:
  0.6 66.4 %copy-start = (bf16[384,1536]{1,0:T(8,128)(2,1)S(1)}, bf16[384,1536]{1,0:T(8,128)(2,1)}, u32[]{:S(2)}) copy-start(bf16[384,1536]{1,0:T(8,128)(2,1)} %param.5) | copy-start | bytes 3538948
  0.6 12.8 %collective-permute-start = (bf16[256,1536]{1,0:T(8,128)(2,1)}, bf16[256,1536]{1,0:T(8,128)(2,1)S(1)}, u32[]{:S(2)}, u32[]{:S(2)}) collective-permute-start(bf16[256,1536]{1,0:T(8,128)(2,1)} %param.3), channel_id=1, source_target_pairs={{0,1},{1,2},{2,3},{3,4},{4,5},{5,6},{6,7},{7,0},{8,9},{9,10},{10,1... | collective-permute-start | bytes 2359304 | tf_op jit(solution)/shard_map/ppermute | solution.py:81
  0.7 12.8 %collective-permute-start.1 = (bf16[256,1536]{1,0:T(8,128)(2,1)}, bf16[256,1536]{1,0:T(8,128)(2,1)}, u32[]{:S(2)}, u32[]{:S(2)}) collective-permute-start(bf16[256,1536]{1,0:T(8,128)(2,1)} %param.3), channel_id=1, source_target_pairs={{0,7},{1,0},{2,1},{3,2},{4,3},{5,4},{6,5},{7,6},{8,15},{9,8},{10,9... | collective-permute-start | bytes 2359304 | tf_op jit(solution)/shard_map/ppermute | solution.py:84
  13.5 15.3 %copy-start.3 = (bf16[256,1536]{1,0:T(8,128)(2,1)}, bf16[256,1536]{1,0:T(8,128)(2,1)S(1)}, u32[]{:S(2)}) copy-start(bf16[256,1536]{1,0:T(8,128)(2,1)S(1)} %collective-permute-done) | copy-start | bytes 2359300
  13.5 12.7 %collective-permute-start.2 = (bf16[256,1536]{1,0:T(8,128)(2,1)S(1)}, bf16[256,1536]{1,0:T(8,128)(2,1)}, u32[]{:S(2)}, u32[]{:S(2)}) collective-permute-start(bf16[256,1536]{1,0:T(8,128)(2,1)S(1)} %collective-permute-done), channel_id=1, source_target_pairs={{0,1},{1,2},{2,3},{3,4},{4,5},{5,6},{6,7},{7,0},{8,9},{9,10},{10,1... | collective-permute-start | bytes 2359304 | tf_op jit(solution)/shard_map/ppermute | solution.py:81
  13.5 21.0 %collective-permute-start.3 = (bf16[256,1536]{1,0:T(8,128)(2,1)}, bf16[256,1536]{1,0:T(8,128)(2,1)}, u32[]{:S(2)}, u32[]{:S(2)}) collective-permute-start(bf16[256,1536]{1,0:T(8,128)(2,1)} %collective-permute-done.1), channel_id=1, source_target_pairs={{0,7},{1,0},{2,1},{3,2},{4,3},{5,4},{6,5},{7,6},{8,15},{9,8},{10,9... | collective-permute-start | bytes 2359304 | tf_op jit(solution)/shard_map/ppermute | solution.py:84
  26.2 16.2 %collective-permute-start.4 = (bf16[256,1536]{1,0:T(8,128)(2,1)}, bf16[256,1536]{1,0:T(8,128)(2,1)S(1)}, u32[]{:S(2)}, u32[]{:S(2)}) collective-permute-start(bf16[256,1536]{1,0:T(8,128)(2,1)} %collective-permute-done.2), channel_id=1, source_target_pairs={{0,1},{1,2},{2,3},{3,4},{4,5},{5,6},{6,7},{7,0},{8,9},{9,10},{10,1... | collective-permute-start | bytes 2359304 | tf_op jit(solution)/shard_map/ppermute | solution.py:81
  28.8 42.8 %all-to-all-start.1 = ((bf16[256,8,384]{0,2,1:T(8,128)(2,1)}), bf16[256,8,384]{0,2,1:T(8,128)(2,1)S(1)}, u32[]{:S(2)}, u32[]{:S(2)}) async-start(bf16[256,8,384]{0,2,1:T(8,128)(2,1)} %bitcast.11), calls=%async_computation.1 | async-start | bytes 3145728 | tf_op jit(solution)/shard_map/all_to_all | solution.py:89
  33.0 1.1 copy-start.2
  33.0 1.4 copy-start.4
  34.5 25.0 %collective-permute-start.5 = (bf16[256,1536]{1,0:T(8,128)(2,1)}, bf16[256,1536]{1,0:T(8,128)(2,1)S(1)}, u32[]{:S(2)}, u32[]{:S(2)}) collective-permute-start(bf16[256,1536]{1,0:T(8,128)(2,1)} %collective-permute-done.3), channel_id=1, source_target_pairs={{0,7},{1,0},{2,1},{3,2},{4,3},{5,4},{6,5},{7,6},{8,15},{9,8},{10,9... | collective-permute-start | bytes 2359304 | tf_op jit(solution)/shard_map/ppermute | solution.py:84
  42.4 21.9 %collective-permute-start.6 = (bf16[256,1536]{1,0:T(8,128)(2,1)S(1)}, bf16[256,1536]{1,0:T(8,128)(2,1)S(1)}, u32[]{:S(2)}, u32[]{:S(2)}) collective-permute-start(bf16[256,1536]{1,0:T(8,128)(2,1)S(1)} %collective-permute-done.4), channel_id=1, source_target_pairs={{0,1},{1,2},{2,3},{3,4},{4,5},{5,6},{6,7},{7,0},{8,9},{9,10},{10,1... | collective-permute-start | bytes 2359304 | tf_op jit(solution)/shard_map/ppermute | solution.py:81
  64.4 2.7 %copy-start.1 = (bf16[2048,1536]{1,0:T(8,128)(2,1)}, bf16[2048,1536]{1,0:T(8,128)(2,1)S(1)}, u32[]{:S(2)}) copy-start(bf16[2048,1536]{1,0:T(8,128)(2,1)S(1)} %constant_dynamic-update-slice_fusion) | copy-start | bytes 18874372
  71.6 44.7 %all-to-all-start = ((bf16[4,512,384]{2,1,0:T(8,128)(2,1)}), bf16[4,512,384]{2,1,0:T(8,128)(2,1)}, u32[]{:S(2)}, u32[]{:S(2)}) async-start(bf16[4,512,384]{2,1,0:T(8,128)(2,1)} %bitcast.17), calls=%async_computation | async-start | bytes 3145728 | tf_op jit(solution)/shard_map/all_to_all | solution.py:18
  158.0 28.1 %all-to-all-start.3 = ((bf16[8,256,384]{2,1,0:T(8,128)(2,1)}), bf16[8,256,384]{2,1,0:T(8,128)(2,1)S(1)}, u32[]{:S(2)}, u32[]{:S(2)}) async-start(bf16[8,256,384]{2,1,0:T(8,128)(2,1)} %bitcast.13), calls=%async_computation.3 | async-start | bytes 3145728 | tf_op jit(solution)/shard_map/all_to_all | solution.py:92
